TPU v7x, 32 devices: a whole 2x2x4 slice. The times are simulated.
32 devices in a mesh: rep: 4 (over y, x), col: 8 (over z, core).
Axes of the slice: x: 2, y: 2, z: 4, core: 2. Of those that a mesh axis runs over, the one named last changes fastest.
Arguments:
- tables: float32 [2, 256, 32768], P(None, 'col', 'rep'), may hold values from -4 to 4
- accumulator: float32 [2, 32768], P(None, 'rep'), may hold values from 0.1 to 20
- replica_grads: bfloat16 [4, 2, 256, 16384], P('rep', None, 'col'), may hold values from -6 to 6
- block_ids: int32 [2, 128], replicated, may hold values from 0 to 255, as said below
Outputs:
- new_tables: float32 [2, 256, 32768], P(None, 'col', 'rep')
- new_accumulator: float32 [2, 32768], P(None, 'rep')
Inputs may be any that keep to these rules, and one draw needn't show every extreme that they name: `block_ids`: the block ids of one table are distinct; each names a block of 128 rows. Splitting the 32768 rows into 4 equal runs, each run holds exactly 32 of a table's touched blocks.
All inputs are finite; a program needn't handle non-finite values.
Results may differ from a plain program's by a relative error of at most 0.0003.
Values sent between devices are 32-bit elements; how exact they have to be, the bound alone decides.
A program may use at most 64 MiB of HBM per device.

v0:
```python
import jax
import jax.numpy as jnp
from jax import lax
from jax.sharding import PartitionSpec as P

DIM = 256
BLOCK = 128


def row_squares(total):
    return lax.psum(jnp.sum(total * total, axis=1), "col")


def body(tables, accumulator, replica_grads, block_ids):
    own_grad = replica_grads[0].astype(jnp.float32)
    ntab, width, local_rows = tables.shape
    local_blocks = local_rows // BLOCK
    offset = lax.axis_index("rep") * local_blocks
    full_blocks = own_grad.shape[2] // BLOCK
    per_owner = full_blocks // lax.axis_size("rep")
    arranged = []
    owned_ids = []
    for table in range(ntab):
        owner = block_ids[table] // local_blocks
        order = jnp.argsort(owner, stable=True)
        grouped = own_grad[table].reshape(width, full_blocks, BLOCK)
        arranged.append(jnp.take(grouped, order, axis=1).reshape(width, full_blocks * BLOCK))
        sorted_ids = jnp.take(block_ids[table], order, axis=0)
        owned_ids.append(
            lax.dynamic_slice_in_dim(sorted_ids, lax.axis_index("rep") * per_owner, per_owner)
        )
    total = lax.psum_scatter(jnp.stack(arranged), "rep", scatter_dimension=2, tiled=True)
    squares = row_squares(total)
    used_ids = jnp.stack(owned_ids)
    slab = total.shape[2]
    nblk = slab // BLOCK
    blocked = tables.reshape(ntab, width, local_blocks, BLOCK)
    acc_blocked = accumulator.reshape(ntab, local_blocks, BLOCK)
    out_tab = []
    out_acc = []
    for table in range(ntab):
        local_ids = used_ids[table] - offset
        inside = (local_ids >= 0) & (local_ids < local_blocks)
        safe_ids = jnp.where(inside, local_ids, 0)
        target = jnp.where(inside, local_ids, local_blocks)
        old_rows = jnp.take(blocked[table], safe_ids, axis=1).reshape(width, slab)
        old_accum = jnp.take(acc_blocked[table], safe_ids, axis=0).reshape(slab)
        fresh = old_accum + squares[table] / DIM
        moved = old_rows - 0.1 * total[table] / (jnp.sqrt(fresh)[None, :] + 1e-08)
        new_blocks = (
            blocked[table].at[:, target].set(moved.reshape(width, nblk, BLOCK), mode="drop")
        )
        new_acc = acc_blocked[table].at[target].set(fresh.reshape(nblk, BLOCK), mode="drop")
        out_tab.append(new_blocks.reshape(width, local_rows))
        out_acc.append(new_acc.reshape(local_rows))
    return (jnp.stack(out_tab), jnp.stack(out_acc))


def solution(mesh):
    return jax.shard_map(
        body,
        mesh=mesh,
        in_specs=(P(None, "col", "rep"), P(None, "rep"), P("rep", None, "col", None), P()),
        out_specs=(P(None, "col", "rep"), P(None, "rep")),
        check_vma=False,
    )
```

profile of v0, /device:TPU:0, one launch (start us, length us, event | category | flops | bytes accessed | tf_op | source)
XLA Modules:
  0.0 150.6 jit_solution(7778629519587096425)
XLA Ops:
  8.7 2.5 %sort.31 = (s32[128]{0:T(128)}, s32[128]{0:T(128)S(1)}) sort(s32[128]{0:T(128)S(1)} %get-tuple-element.32, s32[128]{0:T(128)S(1)} %iota.7), dimensions={0}, to_apply=%region_0.1 | sort | flops 896 | bytes 2048 | tf_op jit(solution)/shard_map/jit(argsort)/sort | solution.py:25
  11.3 1.2 gather_fusion
  12.5 2.5 %sort.32 = (s32[128]{0:T(128)}, s32[128]{0:T(128)S(1)}) sort(s32[128]{0:T(128)S(1)} %get-tuple-element.33, s32[128]{0:T(128)S(1)} %iota.8), dimensions={0}, to_apply=%region_1.0 | sort | flops 896 | bytes 2048 | tf_op jit(solution)/shard_map/jit(argsort)/sort | solution.py:25
  15.1 1.2 gather_fusion.5
  16.3 1.9 %convert_element_type.4 = f32[1,2,32,16384]{3,2,1,0:T(8,128)S(1)} convert(bf16[1,2,32,16384]{3,2,1,0:T(8,128)(2,1)} %param.14) | non-fusion elementwise | flops 1048576 | bytes 6291456 | tf_op jit(solution)/shard_map/convert_element_type | solution.py:15
  18.2 1.6 %slice_bitcast_fusion.1 = (f32[4,8,128,128]{3,1,2,0:T(8,128)S(1)}, f32[4,8,128,128]{3,1,2,0:T(8,128)}) fusion(f32[1,2,32,16384]{3,2,1,0:T(8,128)S(1)} %convert_element_type.4), kind=kLoop, calls=%fused_computation.14 | loop fusion | bytes 8388608
  20.2 2.6 %copy.13 = f32[32,128,128]{2,0,1:T(8,128)} copy(f32[32,128,128]{2,1,0:T(8,128)S(1)} %bitcast.60) | data formatting | bytes 4194304 | tf_op jit(solution)/shard_map/reshape;squeeze | solution.py:26
  22.8 2.3 %gather_fusion.2 = f32[128,32,128]{2,1,0:T(8,128)S(1)} fusion(f32[32,128,128]{2,0,1:T(8,128)} %copy.13, s32[1024]{0:T(1024)S(1)} %pad_clamp_fusion.3), kind=kCustom, calls=%fused_computation.2.clone | custom fusion | bytes 4194816 | tf_op jit(solution)/shard_map/jit(_take)/gather | solution.py:27
  25.3 1.2 copy.14
  26.5 1.5 %stack_reshape.18 = f32[1,32,16384]{2,1,0:T(8,128)} reshape(f32[32,128,128]{2,1,0:T(8,128)S(1)} %copy.14) | data formatting | bytes 4194304 | tf_op jit(solution)/shard_map/stack;reshape | solution.py:32
  28.0 2.0 %copy.26 = f32[4,8,128,128]{3,2,1,0:T(8,128)S(1)} copy(f32[4,8,128,128]{3,1,2,0:T(8,128)} %get-tuple-element.19) | data formatting | bytes 4194304
  30.0 2.5 %copy.15 = f32[32,128,128]{2,0,1:T(8,128)} copy(f32[32,128,128]{2,1,0:T(8,128)S(1)} %bitcast.61) | data formatting | bytes 4194304 | tf_op jit(solution)/shard_map/reshape;squeeze | solution.py:26
  32.5 2.3 %gather_fusion.3 = f32[128,32,128]{2,1,0:T(8,128)S(1)} fusion(f32[32,128,128]{2,0,1:T(8,128)} %copy.15, s32[1024]{0:T(1024)S(1)} %pad_clamp_fusion.1), kind=kCustom, calls=%fused_computation.6.clone | custom fusion | bytes 4194816 | tf_op jit(solution)/shard_map/jit(_take)/gather | solution.py:27
  36.3 1.5 %stack_reshape.19 = f32[1,32,16384]{2,1,0:T(8,128)} reshape(f32[32,128,128]{2,1,0:T(8,128)S(1)} %copy.16) | data formatting | bytes 4194304 | tf_op jit(solution)/shard_map/stack;reshape | solution.py:32
  37.8 4.4 %pad_maximum_fusion = f32[2,32,16384]{2,1,0:T(8,128)} fusion(f32[1,32,16384]{2,1,0:T(8,128)} %stack_reshape.19, f32[1,32,16384]{2,1,0:T(8,128)} %stack_reshape.18), kind=kLoop, calls=%fused_computation.12 | loop fusion | flops 1048576 | bytes 8388608 | tf_op jit(solution)/shard_map/stack | solution.py:32
  42.3 1.7 %slice_bitcast_fusion.3 = (f32[4,8,64,128]{3,1,2,0:T(8,128)S(1)}, f32[4,8,64,128]{3,1,2,0:T(8,128)S(1)}) fusion(f32[2,32,8192]{2,1,0:T(8,128)} %param.12), kind=kLoop, calls=%fused_computation.20 | loop fusion | bytes 4194304
  47.5 1.4 gather_fusion.6
  49.2 48.6 %reduce-scatter.2.cloned.1.call-done = f32[2,32,4096]{2,1,0:T(8,128)} async-done(((f32[2,32,16384]{2,1,0:T(8,128)}), f32[2,32,4096]{2,1,0:T(8,128)}) %reduce-scatter.2.cloned.1.call-update) | async-done | bytes 1048592 | tf_op jit(solution)/shard_map/reduce_scatter | solution.py:32
  97.7 1.4 multiply_reduce_fusion
  99.1 28.4 %psum.7 = f32[2,4096]{1,0:T(2,128)S(1)} all-reduce(f32[2,4096]{1,0:T(2,128)S(1)} %multiply_reduce_fusion), channel_id=1, replica_groups=mesh['rep'=4,'col'=8] {'col'}, use_global_device_ids=true, to_apply=%region_4.9 | all-reduce | flops 8192 | bytes 65536 | tf_op jit(solution)/shard_map/psum | solution.py:11
  127.5 2.1 %fusion.1 = (f32[4,8,32,128]{3,1,2,0:T(8,128)S(1)}, f32[4,8,32,128]{3,1,2,0:T(8,128)}) fusion(f32[2,32,4096]{2,1,0:T(8,128)} %reduce-scatter.2.cloned.1.call-done), kind=kLoop, calls=%fused_computation.24 | loop fusion | flops 262144 | bytes 2097152
  131.8 3.4 %scatter_fusion = f32[32,64,128]{2,0,1:T(8,128)S(1)} fusion(f32[32,64,128]{2,0,1:T(8,128)S(1)} %copy.18, s32[32]{0:T(128)S(1)} %get-tuple-element.35, f32[32,32,128]{2,1,0:T(8,128)} %fusion.3), kind=kCustom, calls=%fused_computation.8 | custom fusion | bytes 1572992 | tf_op jit(solution)/shard_map/scatter | solution.py:51
  139.2 1.5 %scatter_fusion.1 = f32[32,64,128]{2,0,1:T(8,128)S(1)} fusion(f32[32,64,128]{2,0,1:T(8,128)S(1)} %copy.22, s32[32]{0:T(128)S(1)} %get-tuple-element.34, f32[32,32,128]{2,1,0:T(8,128)S(1)} %fusion.2), kind=kCustom, calls=%fused_computation.9 | custom fusion | bytes 1572992 | tf_op jit(solution)/shard_map/scatter | solution.py:51
  142.3 1.5 pad_maximum_fusion.1
  (48 shorter events, 15.1 us)
Async XLA Ops:
  7.2 90.6 %reduce-scatter.2.cloned.1.call-start = ((), (), s32[]{:S(2)}) async-start(), calls=%async_computation.1 | async-start | bytes 5242880 | tf_op jit(solution)/shard_map/reduce_scatter | solution.py:32
  44.0 0.9 copy-start.2
  135.7 3.1 %copy-start.1 = (f32[32,32,128]{2,1,0:T(8,128)S(1)}, f32[32,32,128]{2,1,0:T(8,128)}, u32[]{:S(2)}) copy-start(f32[32,32,128]{2,1,0:T(8,128)} %gather_fusion.6) | copy-start | bytes 1572868
  140.7 1.5 %copy-start = (f32[1,32,8192]{2,1,0:T(8,128)S(1)}, f32[1,32,8192]{2,1,0:T(8,128)}, u32[]{:S(2)}) copy-start(f32[1,32,8192]{2,1,0:T(8,128)} %stack_reshape.20) | copy-start | bytes 3145732
Sparse Core Ops, SparseCore 0:
  42.4 55.3 reduce-scatter.1
where the time goes:
time: 151 us
  waiting for transfers between devices  48.6 us (32%)
  local copies, waits for them, and re-layouts  37.5 us (25%)
  blocking collectives  28.4 us (19%)
  other arithmetic  21.7 us (14%)
  between operations  14.3 us (9%)
    reduce_scatter x1, waiting for transfers between devices, body(): lax.psum_scatter(jnp.stack(arranged), 'rep', scatter_dimension=2, tiled=T...  48.6 us
    psum x1, blocking collectives, row_squares(): return lax.psum(jnp.sum(total * total, axis=1), 'col')  28.4 us
    unnamed x14, local copies, waits for them, and re-layouts  7.26 us
    scatter x4, local copies, waits for them, and re-layouts, body(): blocked[table].at[:, target]  6.1 us
    another operation x2, local copies, waits for them, and re-layouts, body(): grouped = own_grad[table].reshape(width, full_blocks, BLOCK)  5.11 us
    sort x2, other arithmetic, body(): order = jnp.argsort(owner, stable=True)  5.07 us
    gather x2, local copies, waits for them, and re-layouts, body(): jnp.take(grouped, order, axis=1).reshape(width, full_blocks * BLOCK)  4.54 us
    another operation x1, other arithmetic, body(): jnp.stack(arranged)  4.45 us
  transfers between devices with their start and end apart: 1, of which 1 were waited for; matrix products, arithmetic and copies ran while one was open for 5% of the time, Pallas kernels for 0%

commit v1 on v0

--- a/solution.py
+++ b/solution.py
@@ -8,7 +8,7 @@
 
 
 def row_squares(total):
-    return lax.psum(jnp.sum(total * total, axis=1), "col")
+    return jnp.sum(lax.all_gather(jnp.sum(total * total, axis=1), "col"), axis=0)
 
 
 def body(tables, accumulator, replica_grads, block_ids):

time: 151 us -> 138 us (0.914)
  blocking collectives: 28.4 us -> 14.4 us
  other arithmetic: 21.7 us -> 23.3 us
    psum x1 -> x0, blocking collectives: 28.4 us -> none  [row_squares(): return lax.psum(jnp.sum(total * total, axis=1), 'col')]
    all_gather x0 -> x1, blocking collectives: none -> 14.4 us  [row_squares(): lax.all_gather(jnp.sum(total * total, axis=1), 'col')]
    unnamed x14 -> x24, local copies, waits for them, and re-layouts: 7.26 us -> 7.28 us
  transfers between devices with their start and end apart: 1 -> 1, of which waited for: 1 -> 1; matrix products, arithmetic and copies ran while one was open for 5% -> 6% of each run, Pallas kernels for 0% -> 0%
where the time goes in v1:
time: 138 us; the launch traced here: 137 us
  waiting for transfers between devices  47.5 us (34%)
  local copies, waits for them, and re-layouts  37.6 us (27%)
  other arithmetic  23.3 us (17%)
  blocking collectives  14.4 us (10%)
  between operations  14.4 us (10%)
    reduce_scatter x1, waiting for transfers between devices, body(): lax.psum_scatter(jnp.stack(arranged), 'rep', scatter_dimension=2, tiled=T...  47.4 us
    all_gather x1, blocking collectives, row_squares(): lax.all_gather(jnp.sum(total * total, axis=1), 'col')  14.4 us
    unnamed x24, local copies, waits for them, and re-layouts  7.28 us
    scatter x4, local copies, waits for them, and re-layouts, body(): blocked[table].at[:, target]  6.23 us
    another operation x2, local copies, waits for them, and re-layouts, body(): grouped = own_grad[table].reshape(width, full_blocks, BLOCK)  5.11 us
    sort x2, other arithmetic, body(): order = jnp.argsort(owner, stable=True)  5.07 us
    gather x2, local copies, waits for them, and re-layouts, body(): jnp.take(grouped, order, axis=1).reshape(width, full_blocks * BLOCK)  4.54 us
    another operation x1, other arithmetic, body(): jnp.stack(arranged)  4.45 us
  transfers between devices with their start and end apart: 1, of which 1 were waited for; matrix products, arithmetic and copies ran while one was open for 6% of the time, Pallas kernels for 0%

profile of v1, /device:TPU:0, one launch (start us, length us, event | category | flops | bytes accessed | tf_op | source)
XLA Modules:
  0.0 137.2 jit_solution(9000679372514960082)
XLA Ops:
  8.7 2.5 %sort.31 = (s32[128]{0:T(128)}, s32[128]{0:T(128)S(1)}) sort(s32[128]{0:T(128)S(1)} %get-tuple-element.32, s32[128]{0:T(128)S(1)} %iota.7), dimensions={0}, to_apply=%region_0.1 | sort | flops 896 | bytes 2048 | tf_op jit(solution)/shard_map/jit(argsort)/sort | solution.py:25
  11.3 1.2 gather_fusion
  12.5 2.5 %sort.32 = (s32[128]{0:T(128)}, s32[128]{0:T(128)S(1)}) sort(s32[128]{0:T(128)S(1)} %get-tuple-element.33, s32[128]{0:T(128)S(1)} %iota.8), dimensions={0}, to_apply=%region_1.0 | sort | flops 896 | bytes 2048 | tf_op jit(solution)/shard_map/jit(argsort)/sort | solution.py:25
  15.1 1.2 gather_fusion.5
  16.3 1.9 %convert_element_type.4 = f32[1,2,32,16384]{3,2,1,0:T(8,128)S(1)} convert(bf16[1,2,32,16384]{3,2,1,0:T(8,128)(2,1)} %param.14) | non-fusion elementwise | flops 1048576 | bytes 6291456 | tf_op jit(solution)/shard_map/convert_element_type | solution.py:15
  18.2 1.6 %slice_bitcast_fusion.1 = (f32[4,8,128,128]{3,1,2,0:T(8,128)S(1)}, f32[4,8,128,128]{3,1,2,0:T(8,128)}) fusion(f32[1,2,32,16384]{3,2,1,0:T(8,128)S(1)} %convert_element_type.4), kind=kLoop, calls=%fused_computation.14 | loop fusion | bytes 8388608
  20.2 2.6 %copy.25 = f32[32,128,128]{2,0,1:T(8,128)} copy(f32[32,128,128]{2,1,0:T(8,128)S(1)} %bitcast.61) | data formatting | bytes 4194304 | tf_op jit(solution)/shard_map/reshape;squeeze | solution.py:26
  22.8 2.3 %gather_fusion.2 = f32[128,32,128]{2,1,0:T(8,128)S(1)} fusion(f32[32,128,128]{2,0,1:T(8,128)} %copy.25, s32[1024]{0:T(1024)S(1)} %pad_clamp_fusion.3), kind=kCustom, calls=%fused_computation.2.clone | custom fusion | bytes 4194816 | tf_op jit(solution)/shard_map/jit(_take)/gather | solution.py:27
  25.3 1.2 copy.26
  26.5 1.5 %stack_reshape.18 = f32[1,32,16384]{2,1,0:T(8,128)} reshape(f32[32,128,128]{2,1,0:T(8,128)S(1)} %copy.26) | data formatting | bytes 4194304 | tf_op jit(solution)/shard_map/stack;reshape | solution.py:32
  28.0 2.0 %copy.38 = f32[4,8,128,128]{3,2,1,0:T(8,128)S(1)} copy(f32[4,8,128,128]{3,1,2,0:T(8,128)} %get-tuple-element.19) | data formatting | bytes 4194304
  30.0 2.5 %copy.27 = f32[32,128,128]{2,0,1:T(8,128)} copy(f32[32,128,128]{2,1,0:T(8,128)S(1)} %bitcast.62) | data formatting | bytes 4194304 | tf_op jit(solution)/shard_map/reshape;squeeze | solution.py:26
  32.5 2.3 %gather_fusion.3 = f32[128,32,128]{2,1,0:T(8,128)S(1)} fusion(f32[32,128,128]{2,0,1:T(8,128)} %copy.27, s32[1024]{0:T(1024)S(1)} %pad_clamp_fusion.1), kind=kCustom, calls=%fused_computation.6.clone | custom fusion | bytes 4194816 | tf_op jit(solution)/shard_map/jit(_take)/gather | solution.py:27
  36.3 1.5 %stack_reshape.19 = f32[1,32,16384]{2,1,0:T(8,128)} reshape(f32[32,128,128]{2,1,0:T(8,128)S(1)} %copy.28) | data formatting | bytes 4194304 | tf_op jit(solution)/shard_map/stack;reshape | solution.py:32
  37.8 4.4 %pad_maximum_fusion = f32[2,32,16384]{2,1,0:T(8,128)} fusion(f32[1,32,16384]{2,1,0:T(8,128)} %stack_reshape.19, f32[1,32,16384]{2,1,0:T(8,128)} %stack_reshape.18), kind=kLoop, calls=%fused_computation.12 | loop fusion | flops 1048576 | bytes 8388608 | tf_op jit(solution)/shard_map/stack | solution.py:32
  42.3 1.7 %slice_bitcast_fusion.3 = (f32[4,8,64,128]{3,1,2,0:T(8,128)S(1)}, f32[4,8,64,128]{3,1,2,0:T(8,128)S(1)}) fusion(f32[2,32,8192]{2,1,0:T(8,128)} %param.12), kind=kLoop, calls=%fused_computation.20 | loop fusion | bytes 4194304
  47.6 1.4 %gather_fusion.6 = f32[32,32,128]{2,1,0:T(8,128)} fusion(f32[32,64,128]{2,0,1:T(8,128)S(1)} %copy.34, s32[1024]{0:T(1024)S(1)} %pad_clamp_fusion), kind=kCustom, calls=%fused_computation.5.clone | custom fusion | bytes 1048704 | tf_op jit(solution)/shard_map/jit(_take)/gather | solution.py:46
  50.3 47.4 %reduce-scatter.2.cloned.1.call-done = f32[2,32,4096]{2,1,0:T(8,128)} async-done(((f32[2,32,16384]{2,1,0:T(8,128)}), f32[2,32,4096]{2,1,0:T(8,128)}) %reduce-scatter.2.cloned.1.call-update) | async-done | bytes 1048592 | tf_op jit(solution)/shard_map/reduce_scatter | solution.py:32
  97.8 1.5 %multiply_reduce_fusion = f32[2,4096]{1,0:T(2,128)S(1)} fusion(f32[2,32,4096]{2,1,0:T(8,128)} %reduce-scatter.2.cloned.1.call-done), kind=kLoop, calls=%fused_computation.19 | loop fusion | flops 516096 | bytes 1081344 | tf_op jit(solution)/shard_map/reduce_sum | solution.py:11
  99.2 14.4 %all-gather.1 = f32[8,2,4096]{2,1,0:T(2,128)S(1)} all-gather(f32[1,2,4096]{2,1,0:T(2,128)S(1)} %bitcast.73), channel_id=2, replica_groups=mesh['rep'=4,'col'=8] {'col'}, dimensions={0}, use_global_device_ids=true | all-gather | bytes 294912 | tf_op jit(solution)/shard_map/all_gather | solution.py:11
  116.5 1.8 %fusion.3 = f32[32,32,128]{2,1,0:T(8,128)} fusion(f32[32,32,128]{2,1,0:T(8,128)S(1)} %bitcast.65, f32[32,32,128]{2,1,0:T(8,128)S(1)} %gather_fusion.1, f32[32,128]{1,0:T(8,128)S(1)} %bitcast.75, pred[32]{0:T(512)(128)(4,1)} %copy-done.6), kind=kLoop, calls=%fused_computation.28 | loop fusion | flops 393216 | bytes 1589280 | tf_op jit(solution)/shard_map/sub | solution.py:49
  118.3 3.5 %scatter_fusion = f32[32,64,128]{2,0,1:T(8,128)S(1)} fusion(f32[32,64,128]{2,0,1:T(8,128)S(1)} %copy.30, s32[32]{0:T(128)} %get-tuple-element.35, f32[32,32,128]{2,1,0:T(8,128)} %fusion.3), kind=kCustom, calls=%fused_computation.8 | custom fusion | bytes 1572992 | tf_op jit(solution)/shard_map/scatter | solution.py:51
  125.9 1.5 %scatter_fusion.1 = f32[32,64,128]{2,0,1:T(8,128)S(1)} fusion(f32[32,64,128]{2,0,1:T(8,128)S(1)} %copy.34, s32[32]{0:T(128)S(1)} %copy-done.7, f32[32,32,128]{2,1,0:T(8,128)S(1)} %fusion.2), kind=kCustom, calls=%fused_computation.9 | custom fusion | bytes 1572992 | tf_op jit(solution)/shard_map/scatter | solution.py:51
  128.9 1.5 %pad_maximum_fusion.1 = f32[2,32,8192]{2,1,0:T(8,128)} fusion(f32[1,32,8192]{2,1,0:T(8,128)S(1)} %stack_reshape.21, f32[1,32,8192]{2,1,0:T(8,128)S(1)} %copy-done.1), kind=kLoop, calls=%fused_computation.15 | loop fusion | flops 524288 | bytes 4194304 | tf_op jit(solution)/shard_map/stack | solution.py:56
  (59 shorter events, 16.9 us)
Async XLA Ops:
  7.2 90.6 %reduce-scatter.2.cloned.1.call-start = ((), (), s32[]{:S(2)}) async-start(), calls=%async_computation.1 | async-start | bytes 5242880 | tf_op jit(solution)/shard_map/reduce_scatter | solution.py:32
  44.0 0.9 copy-start.3
  44.9 4.7 %copy-start.4 = (pred[32]{0:T(512)(128)(4,1)}, pred[32]{0:T(512)(128)(4,1)S(1)}, u32[]{:S(2)}) copy-start(pred[32]{0:T(512)(128)(4,1)S(1)} %get-tuple-element.14) | copy-start | bytes 100
  44.9 4.7 %copy-start.6 = (pred[32]{0:T(512)(128)(4,1)}, pred[32]{0:T(512)(128)(4,1)S(1)}, u32[]{:S(2)}) copy-start(pred[32]{0:T(512)(128)(4,1)S(1)} %get-tuple-element.36) | copy-start | bytes 100
  97.7 15.9 %copy-start = (f32[2,32,4096]{2,1,0:T(8,128)S(1)}, f32[2,32,4096]{2,1,0:T(8,128)}, u32[]{:S(2)}) copy-start(f32[2,32,4096]{2,1,0:T(8,128)} %reduce-scatter.2.cloned.1.call-done) | copy-start | bytes 3145732
  122.4 2.3 %copy-start.5 = (pred[32]{0:T(512)(128)(4,1)S(1)}, pred[32]{0:T(512)(128)(4,1)}, u32[]{:S(2)}) copy-start(pred[32]{0:T(512)(128)(4,1)} %copy-done.4) | copy-start | bytes 100
  122.4 2.3 %copy-start.7 = (s32[32]{0:T(128)S(1)}, s32[32]{0:T(128)}, u32[]{:S(2)}) copy-start(s32[32]{0:T(128)} %get-tuple-element.34) | copy-start | bytes 388
  122.4 3.1 %copy-start.2 = (f32[32,32,128]{2,1,0:T(8,128)S(1)}, f32[32,32,128]{2,1,0:T(8,128)}, u32[]{:S(2)}) copy-start(f32[32,32,128]{2,1,0:T(8,128)} %gather_fusion.6) | copy-start | bytes 1572868
  127.4 1.5 %copy-start.1 = (f32[1,32,8192]{2,1,0:T(8,128)S(1)}, f32[1,32,8192]{2,1,0:T(8,128)}, u32[]{:S(2)}) copy-start(f32[1,32,8192]{2,1,0:T(8,128)} %stack_reshape.20) | copy-start | bytes 3145732
Sparse Core Ops, SparseCore 0:
  42.4 55.3 reduce-scatter.1
